TPU v7x, 32 devices: a whole 2x2x4 slice. The times are simulated.
32 devices in a mesh: owner: 4 (over x, core), rows: 8 (over z, y).
Axes of the slice: x: 2, y: 2, z: 4, core: 2. Of those that a mesh axis runs over, the one named last changes fastest.
Arguments:
- master_down: float32 [8, 14336, 4096], P('owner', None, 'rows'), may hold values from -0.046875 to 0.046875
- router_weight: float32 [4096, 8], P('rows', 'owner'), may hold values from -0.09375 to 0.09375
- router_gain: float32 [4096], P('rows'), may hold values from 0.25 to 1.75
Outputs:
- final_down: bfloat16 [8, 4096, 14336], P('owner', None, 'rows')
- serve_router: bfloat16 [4096, 8], replicated
All inputs are finite; a program needn't handle non-finite values.
Results may differ from a plain program's by a relative error of at most 0.001.
Values may be sent and summed in bfloat16 or wider, within the bound.
No kernel may reach another device: no remote copies, remote signals or barrier semaphores. Data moves between devices by JAX's collectives and lax.ppermute only.
A program may use at most 192 MiB of HBM per device.

v0:
```python
import jax
import jax.numpy as jnp
from jax import lax
from jax.sharding import PartitionSpec as P


def shards(master_down, router_weight, router_gain):
    turned_down = jnp.transpose(master_down, (0, 2, 1))
    narrow_down = turned_down.astype(jnp.bfloat16)
    final_down = lax.all_to_all(narrow_down, "rows", split_axis=2, concat_axis=1, tiled=True)
    part_router = (router_weight * router_gain[:, None]).astype(jnp.bfloat16)
    row_router = lax.all_gather(part_router, "rows", axis=0, tiled=True)
    serve_router = lax.all_gather(row_router, "owner", axis=1, tiled=True)
    return (final_down, serve_router)


def solution(mesh):
    return jax.shard_map(
        shards,
        mesh=mesh,
        in_specs=(P("owner", None, "rows"), P("rows", "owner"), P("rows")),
        out_specs=(P("owner", None, "rows"), P()),
        check_vma=False,
    )
```

profile of v0, /device:TPU:0, one launch (start us, length us, event | category | flops | bytes accessed | tf_op | source)
XLA Modules:
  0.0 817.2 jit_solution(17658122797674117112)
XLA Ops:
  0.6 28.5 %convert_element_type.12 = bf16[2,14336,512]{2,1,0:T(8,128)(2,1)} convert(f32[2,14336,512]{2,1,0:T(8,128)} %param.3) | non-fusion elementwise | flops 14680064 | bytes 88080384 | tf_op jit(solution)/shard_map/convert_element_type | solution.py:9
  29.1 52.8 %copy.10 = bf16[2,14336,512]{2,0,1:T(2,128)(2,1)} copy(bf16[2,14336,512]{2,1,0:T(8,128)(2,1)} %convert_element_type.12) | data formatting | bytes 58720256
  81.9 0.0 copy-start
  81.9 0.0 copy-start.1
  81.9 7.5 all-to-all-start
  89.4 0.0 copy-done
  89.4 0.0 copy-done.1
  89.4 652.0 %all_gather.6 = bf16[4096,2]{0,1:T(2,128)(2,1)S(1)} all-gather(bf16[512,2]{0,1:T(2,128)(2,1)S(1)} %multiply_convert_fusion), channel_id=1, replica_groups=mesh['owner'=4,'rows'=8] {'rows'}, dimensions={0}, use_global_device_ids=true | all-gather | bytes 18432 | tf_op jit(solution)/shard_map/all_gather | solution.py:12
  741.4 5.2 all-gather
  746.6 0.7 reshape.6
  747.2 0.0 all-to-all-done
  747.3 70.0 %copy.7 = bf16[2,8,512,1792]{3,2,1,0:T(8,128)(2,1)} copy(bf16[2,8,512,1792]{2,0,3,1:T(2,128)(2,1)} %bitcast.2) | data formatting | bytes 58720256 | tf_op jit(solution)/shard_map/all_to_all | solution.py:10
  (1 shorter events, 0.0 us)
Async XLA Ops:
  81.9 7.5 copy-start
  81.9 7.5 copy-start.1
  81.9 665.3 %all-to-all-start = ((bf16[2,512,14336]{1,0,2:T(2,128)(2,1)}), bf16[2,512,14336]{1,0,2:T(2,128)(2,1)}, u32[]{:S(2)}, u32[]{:S(2)}) async-start(bf16[2,512,14336]{1,0,2:T(2,128)(2,1)} %bitcast.11), calls=%async_computation | async-start | bytes 58720256 | tf_op jit(solution)/shard_map/all_to_all | solution.py:10
where the time goes:
time: 819 us; the launch traced here: 817 us
  blocking collectives  657 us (80%)
  local copies, waits for them, and re-layouts  123 us (15%)
  other arithmetic  28.5 us (3%)
    all_gather x1, blocking collectives, shards(): row_router = lax.all_gather(part_router, 'rows', axis=0, tiled=True)  652 us
    all_to_all x1, local copies, waits for them, and re-layouts, shards(): lax.all_to_all(narrow_down, 'rows', split_axis=2, concat_axis=1, tiled=True)  70 us
    unnamed x6, local copies, waits for them, and re-layouts  53.5 us
    convert_element_type x1, other arithmetic, shards(): narrow_down = turned_down.astype(jnp.bfloat16)  28.5 us
  transfers between devices with their start and end apart: 1, of which 0 were waited for; matrix products, arithmetic and copies ran while one was open for 0% of the time, Pallas kernels for 0%

commit v1 on v0

--- a/solution.py
+++ b/solution.py
@@ -7,7 +7,12 @@
 def shards(master_down, router_weight, router_gain):
     turned_down = jnp.transpose(master_down, (0, 2, 1))
     narrow_down = turned_down.astype(jnp.bfloat16)
-    final_down = lax.all_to_all(narrow_down, "rows", split_axis=2, concat_axis=1, tiled=True)
+    final_down = jnp.concatenate(
+        lax.all_to_all(
+            jnp.stack(jnp.split(narrow_down, lax.axis_size("rows"), axis=2)), "rows", 0, 0
+        ),
+        axis=1,
+    )
     part_router = (router_weight * router_gain[:, None]).astype(jnp.bfloat16)
     row_router = lax.all_gather(part_router, "rows", axis=0, tiled=True)
     serve_router = lax.all_gather(row_router, "owner", axis=1, tiled=True)

time: 819 us -> 765 us (0.934)
  local copies, waits for them, and re-layouts: 123 us -> 69.4 us
    all_to_all x1 -> x0, local copies, waits for them, and re-layouts: 70 us -> none  [shards(): lax.all_to_all(narrow_down, 'rows', split_axis=2, concat_axis=1, tiled=True)]
    reshape x0 -> x1, local copies, waits for them, and re-layouts: none -> 36 us  [shards(): jnp.concatenate(lax.all_to_all(jnp.stack(jnp.split(narrow_down, lax.axis_...]
    unnamed x6 -> x12, local copies, waits for them, and re-layouts: 53.5 us -> 29.4 us
where the time goes in v1:
time: 765 us; the launch traced here: 763 us
  blocking collectives  657 us (86%)
  local copies, waits for them, and re-layouts  69.4 us (9%)
  other arithmetic  28.5 us (4%)
    all_gather x1, blocking collectives, shards(): row_router = lax.all_gather(part_router, 'rows', axis=0, tiled=True)  652 us
    reshape x1, local copies, waits for them, and re-layouts, shards(): jnp.concatenate(lax.all_to_all(jnp.stack(jnp.split(narrow_down, lax.axis_...  36 us
    unnamed x12, local copies, waits for them, and re-layouts  29.4 us
    convert_element_type x1, other arithmetic, shards(): narrow_down = turned_down.astype(jnp.bfloat16)  28.5 us
  transfers between devices with their start and end apart: 1, of which 0 were waited for; matrix products, arithmetic and copies ran while one was open for 0% of the time, Pallas kernels for 0%

profile of v1, /device:TPU:0, one launch (start us, length us, event | category | flops | bytes accessed | tf_op | source)
XLA Modules:
  0.0 763.2 jit_solution(5256674096772135787)
XLA Ops:
  0.6 28.5 %convert_bitcast_fusion = bf16[2,512,14336]{1,2,0:T(8,128)(2,1)} fusion(f32[2,14336,512]{2,1,0:T(8,128)} %param.3), kind=kLoop, calls=%fused_computation | loop fusion | flops 14680064 | bytes 88080384 | tf_op jit(solution)/shard_map/convert_element_type | solution.py:9
  29.1 4.1 fusion.7
  33.1 4.1 fusion.6
  37.2 4.1 fusion.5
  41.3 4.1 fusion.4
  45.4 4.2 fusion.3
  49.6 4.1 fusion.2
  53.6 4.2 fusion.1
  57.8 4.1 fusion
  61.9 0.0 copy-start
  61.9 0.0 copy-start.1
  61.9 7.4 all-to-all-start
  69.3 0.0 copy-done
  69.3 0.0 copy-done.1
  69.4 652.0 %all_gather.6 = bf16[4096,2]{0,1:T(2,128)(2,1)S(1)} all-gather(bf16[512,2]{0,1:T(2,128)(2,1)S(1)} %multiply_convert_fusion), channel_id=1, replica_groups=mesh['owner'=4,'rows'=8] {'rows'}, dimensions={0}, use_global_device_ids=true | all-gather | bytes 18432 | tf_op jit(solution)/shard_map/all_gather | solution.py:17
  721.3 5.2 all-gather
  726.6 0.7 reshape.14
  727.2 0.0 all-to-all-done
  727.2 36.0 %copy.6 = bf16[2,8,512,1792]{3,2,1,0:T(8,128)(2,1)} copy(bf16[2,8,512,1792]{2,3,0,1:T(8,128)(2,1)} %bitcast.9) | data formatting | bytes 58720256 | tf_op jit(solution)/shard_map/reshape | solution.py:10
  (1 shorter events, 0.0 us)
Async XLA Ops:
  61.9 7.4 copy-start
  61.9 7.5 copy-start.1
  61.9 665.3 %all-to-all-start = ((bf16[8,2,512,1792]{2,3,1,0:T(8,128)(2,1)}), bf16[8,2,512,1792]{2,3,1,0:T(8,128)(2,1)}, u32[]{:S(2)}, u32[]{:S(2)}) async-start(bf16[8,2,512,1792]{2,3,1,0:T(8,128)(2,1)} %fusion), calls=%async_computation | async-start | bytes 58720256 | tf_op jit(solution)/shard_map/all_to_all | solution.py:11
